TPU v7x, 512 devices: a whole 4x8x8 slice. The times are simulated.
512 devices in a mesh: resp: 64 (over y, z), head: 8 (over x, core).
Axes of the slice: x: 4, y: 8, z: 8, core: 2. Of those that a mesh axis runs over, the one named last changes fastest.
Arguments:
- queries: bfloat16 [8192, 24576], P('resp', 'head'), may hold values from -8 to 8
- resp_latent: bfloat16 [8192, 576], P('resp'), may hold values from -8 to 8
- prompt_latent: bfloat16 [64, 128, 576], P('resp'), may hold values from -6 to 6
- up_keys: bfloat16 [128, 128, 512], P('head', None, 'resp'), may hold values from -0.5 to 0.5
- up_values: bfloat16 [128, 512, 128], P('head', 'resp'), may hold values from -0.25 to 0.25
- cotangent: bfloat16 [8192, 16384], P('resp', 'head'), may hold values from -6 to 6
- prompt_len: int32 [32], replicated, may hold values from 32 to 128
- resp_len: int32 [128], replicated, may hold values from 16 to 64
- resp_count: int32 [32], replicated, may hold values from 1 to 8, 128 in all
- owner: int32 [32], replicated, may hold values from 0 to 63, as said below
Outputs:
- attended: bfloat16 [8192, 16384], P('resp', 'head')
- grad_queries: bfloat16 [8192, 24576], P('resp', 'head')
- grad_response: float32 [8192, 576], P('resp', 'head')
- grad_prompt: float32 [64, 128, 576], P('resp', None, 'head')
Inputs may be any that keep to these rules, and one draw needn't show every extreme that they name: Distinct slots; prompt p's cache is prompt_latent[owner[p]]. `resp_count`: every prompt has at least one response; they sum to 128.
All inputs are finite; a program needn't handle non-finite values.
Results may differ from a plain program's by a relative error of at most 0.014.
Values may be sent and summed in bfloat16 or wider, within the bound.
No kernel may reach another device: no remote copies, remote signals or barrier semaphores. Data moves between devices by JAX's collectives and lax.ppermute only.
A program may use at most 64 MiB of HBM per device.

v0:
```python
import math
import jax
import jax.numpy as jnp
from jax import lax
from jax.sharding import PartitionSpec as P


def turned_gather(arrays, axis, dims):
    turned = [jnp.moveaxis(a, dim, 0) for a, dim in zip(arrays, dims)]
    both = jnp.concatenate([t.reshape(len(t), -1) for t in turned], axis=1)
    out, at, done = (lax.all_gather(both, axis, axis=0, tiled=True), 0, [])
    for t, dim in zip(turned, dims):
        piece = out[:, at : at + t[0].size].reshape(-1, *t.shape[1:])
        done.append(jnp.moveaxis(piece, 0, dim))
        at += t[0].size
    return tuple(done)


def in_order(tiles, dim):
    tiles = jnp.moveaxis(tiles, 0, dim)
    lengths = tiles.shape
    return tiles.reshape(*lengths[:dim], lengths[dim] * lengths[dim + 1], *lengths[dim + 2 :])


def sent_to_all(array, axis):
    copies = jnp.broadcast_to(array, (lax.axis_size(axis), *array.shape))
    return lax.all_to_all(copies, axis, split_axis=0, concat_axis=0, tiled=True)


def gathered_copies(array, axis, dim):
    return in_order(sent_to_all(array, axis), dim)


def split_up(array, dim, length):
    before, after = (array.shape[:dim], array.shape[dim + 1 :])
    return jnp.moveaxis(array.reshape(*before, length, -1, *after), dim, 0)


def sent_and_summed(array, axis, dim):
    length = lax.axis_size(axis)
    tiles = lax.all_to_all(split_up(array, dim, length), axis, 0, 0, tiled=True)
    return jnp.sum(tiles.astype(jnp.float32), axis=0)


def product(form, left, right):
    return jnp.einsum(form, left, right, preferred_element_type=jnp.float32)


def attend(queries, key_rows, key_valid, row_live, cotangent, up_keys, up_values):
    head_count, nope_width, latent_width = up_keys.shape
    row_count = queries.shape[0]
    split_query = queries.reshape(row_count, head_count, -1)
    score_scale = 1.0 / math.sqrt(split_query.shape[2])
    query_latent = product("thn,hnc->thc", split_query[:, :, :nope_width], up_keys).astype(
        jnp.bfloat16
    )
    query_full = jnp.concatenate([query_latent, split_query[:, :, nope_width:]], axis=2)
    scores = product("thc,kc->thk", query_full, key_rows) * score_scale
    scores = jnp.where(key_valid[:, None, :], scores, -jnp.inf)
    row_max = jnp.max(scores, axis=2, keepdims=True)
    expo = jnp.exp(scores - row_max)
    weights = expo / jnp.sum(expo, axis=2, keepdims=True)
    weights_bf = weights.astype(jnp.bfloat16)
    value_rows = key_rows[:, :latent_width]
    latent_out = product("thk,kc->thc", weights_bf, value_rows).astype(jnp.bfloat16)
    attended = product("thc,hcv->thv", latent_out, up_values) * row_live[:, None, None]
    grad_out = cotangent.reshape(row_count, head_count, -1)
    grad_latent = (product("thv,hcv->thc", grad_out, up_values) * row_live[:, None, None]).astype(
        jnp.bfloat16
    )
    grad_weights = product("thc,kc->thk", grad_latent, value_rows)
    inner = jnp.sum(weights * grad_weights, axis=2, keepdims=True)
    grad_scores = (weights * (grad_weights - inner) * score_scale).astype(jnp.bfloat16)
    grad_full = product("thk,kc->thc", grad_scores, key_rows)
    grad_nope = product(
        "thc,hnc->thn", grad_full[:, :, :latent_width].astype(jnp.bfloat16), up_keys
    )
    grad_query = jnp.concatenate([grad_nope, grad_full[:, :, latent_width:]], axis=2)
    grad_key = product("thk,thc->kc", grad_scores, query_full)
    grad_value = product("thk,thc->kc", weights_bf, grad_latent)
    grad_key = grad_key + jnp.pad(grad_value, ((0, 0), (0, key_rows.shape[1] - latent_width)))
    return (
        attended.reshape(row_count, -1).astype(jnp.bfloat16),
        grad_query.reshape(row_count, -1).astype(jnp.bfloat16),
        grad_key,
    )


def body(
    queries,
    resp_latent,
    prompt_latent,
    up_keys,
    up_values,
    cotangent,
    prompt_len,
    resp_len,
    resp_count,
    owner,
):
    resp_devices = lax.axis_size("resp")
    head_devices = lax.axis_size("head")
    my_index = lax.axis_index("resp")
    head_index = lax.axis_index("head")
    keys_full, values_full = turned_gather((up_keys, up_values), "resp", (2, 1))
    resp_total = resp_len.shape[0]
    per_device = resp_total // resp_devices
    row_count = queries.shape[0] // per_device
    prompt_rows = prompt_latent.shape[1]
    piece_rows = prompt_rows // resp_devices
    latent_cols = prompt_latent.shape[2]
    starts = jnp.cumsum(resp_count) - resp_count
    numbers = jnp.arange(resp_total, dtype=jnp.int32)
    prompt_of = jnp.sum((starts[None, :] <= numbers[:, None]).astype(jnp.int32), axis=1) - 1
    chosen = prompt_of[:, None] == jnp.arange(prompt_len.shape[0], dtype=jnp.int32)[None, :]
    slot_of = jnp.sum(jnp.where(chosen, owner[None, :], 0), axis=1)
    plen_of = jnp.sum(jnp.where(chosen, prompt_len[None, :], 0), axis=1)
    plen_mine = lax.dynamic_slice_in_dim(plen_of, my_index * per_device, per_device)
    rlen_mine = lax.dynamic_slice_in_dim(resp_len, my_index * per_device, per_device)
    col_share = latent_cols // head_devices
    latent_share = lax.dynamic_slice_in_dim(prompt_latent, head_index * col_share, col_share, 2)
    stripes = lax.all_to_all(latent_share, "resp", split_axis=1, concat_axis=0, tiled=True)
    outgoing = jnp.take(stripes, slot_of, axis=0)
    outgoing = outgoing.reshape(resp_devices, per_device, piece_rows, stripes.shape[2])
    fetched = lax.all_to_all(outgoing, "resp", split_axis=0, concat_axis=2, tiled=True)[0]
    fetched = gathered_copies(fetched, "head", 2)
    own_rows = resp_latent.reshape(per_device, row_count, latent_cols)
    key_rows = jnp.concatenate([fetched, own_rows], axis=1)
    positions = jnp.arange(row_count, dtype=jnp.int32)
    prompt_pos = jnp.arange(prompt_rows, dtype=jnp.int32)
    prompt_ok = jnp.broadcast_to(
        prompt_pos[None, None, :] < plen_mine[:, None, None], (per_device, row_count, prompt_rows)
    )
    causal = jnp.broadcast_to(
        positions[None, :, None] >= positions[None, None, :], (per_device, row_count, row_count)
    )
    key_valid = jnp.concatenate([prompt_ok, causal], axis=2)
    row_live = (positions[None, :] < rlen_mine[:, None]).astype(jnp.float32)
    query_blocks = queries.reshape(per_device, row_count, -1)
    grad_blocks = cotangent.reshape(per_device, row_count, -1)
    attended, grad_query, grad_key = jax.vmap(attend, in_axes=(0, 0, 0, 0, 0, None, None))(
        query_blocks, key_rows, key_valid, row_live, grad_blocks, keys_full, values_full
    )
    grad_prompt_rows = grad_key[:, :prompt_rows]
    grad_own = grad_key[:, prompt_rows:].reshape(per_device * row_count, latent_cols)
    grad_prompt_rows, grad_own = (
        sent_and_summed(grad_prompt_rows.astype(jnp.bfloat16), "head", 2),
        sent_and_summed(grad_own.astype(jnp.bfloat16), "head", 1),
    )
    sent_cols = grad_prompt_rows.shape[2]
    arrived = lax.all_to_all(
        grad_prompt_rows[None].astype(jnp.bfloat16), "resp", split_axis=2, concat_axis=0, tiled=True
    ).astype(jnp.float32)
    flat_rows = arrived.reshape(resp_devices * per_device, piece_rows * sent_cols)
    slot_table = (slot_of[None, :] == jnp.arange(resp_devices, dtype=jnp.int32)[:, None]).astype(
        jnp.float32
    )
    summed = jnp.dot(slot_table, flat_rows, precision=lax.Precision.HIGHEST)
    summed = summed.reshape(resp_devices, piece_rows, sent_cols)
    at_owner = lax.all_to_all(
        summed.astype(jnp.bfloat16), "resp", split_axis=0, concat_axis=1, tiled=True
    ).astype(summed.dtype)
    return (
        attended.reshape(per_device * row_count, -1),
        grad_query.reshape(per_device * row_count, -1),
        grad_own,
        at_owner,
    )


def solution(mesh):
    placed = (
        P("resp", "head"),
        P("resp", None),
        P("resp", None, None),
        P("head", None, "resp"),
        P("head", "resp", None),
        P("resp", "head"),
        P(),
        P(),
        P(),
        P(),
    )
    return jax.shard_map(
        body,
        mesh=mesh,
        in_specs=placed,
        out_specs=(
            P("resp", "head"),
            P("resp", "head"),
            P("resp", "head"),
            P("resp", None, "head"),
        ),
        check_vma=False,
    )
```

profile of v0, /device:TPU:1, one launch (start us, length us, event | category | flops | bytes accessed | tf_op | source)
XLA Modules:
  0.0 217.1 jit_solution(1038570056481774946)
XLA Ops:
  7.2 1.5 pad_maximum_fusion.3
  8.8 0.8 copy.159
  9.5 17.1 %all-to-all-start = ((bf16[1,128,72]{2,0,1:T(2,128)(2,1)}), bf16[1,128,72]{2,0,1:T(2,128)(2,1)S(1)}, u32[]{:S(2)}, u32[]{:S(2)}) async-start(bf16[1,128,72]{2,0,1:T(2,128)(2,1)} %copy.159), calls=%async_computation | async-start | bytes 131072 | tf_op jit(solution)/shard_map/all_to_all | solution.py:122
  26.7 0.7 copy.118
  28.3 0.8 select_reduce_fusion.1
  29.4 8.4 %all-to-all-done = bf16[1,128,72]{2,0,1:T(2,128)(2,1)S(1)} async-done(((bf16[1,128,72]{2,0,1:T(2,128)(2,1)}), bf16[1,128,72]{2,0,1:T(2,128)(2,1)S(1)}, u32[]{:S(2)}, u32[]{:S(2)}) %all-to-all-start) | async-done | bytes 18464 | tf_op jit(solution)/shard_map/all_to_all | solution.py:122
  37.8 0.7 gather_fusion
  38.5 0.8 broadcast_select_fusion
  39.4 4.6 %all-to-all-start.1 = ((bf16[64,2,2,72]{3,2,1,0:T(2,128)(2,1)}), bf16[64,2,2,72]{3,2,1,0:T(2,128)(2,1)S(1)}, u32[]{:S(2)}, u32[]{:S(2)}) async-start(bf16[64,2,2,72]{3,2,1,0:T(2,128)(2,1)} %broadcast_select_fusion), calls=%async_computation.1 | async-start | bytes 131072 | tf_op jit(solution)/shard_map/all_to_all | solution.py:125
  44.0 11.2 %all-to-all-done.1 = bf16[64,2,2,72]{3,2,1,0:T(2,128)(2,1)S(1)} async-done(((bf16[64,2,2,72]{3,2,1,0:T(2,128)(2,1)}), bf16[64,2,2,72]{3,2,1,0:T(2,128)(2,1)S(1)}, u32[]{:S(2)}, u32[]{:S(2)}) %all-to-all-start.1) | async-done | bytes 36896 | tf_op jit(solution)/shard_map/all_to_all | solution.py:125
  55.4 0.8 broadcast_in_dim.82
  56.1 7.5 %all-to-all-start.2 = ((bf16[8,2,128,72]{2,3,1,0:T(8,128)(2,1)}), bf16[8,2,128,72]{2,3,1,0:T(8,128)(2,1)}, u32[]{:S(2)}, u32[]{:S(2)}) async-start(bf16[8,2,128,72]{2,3,1,0:T(8,128)(2,1)} %broadcast_in_dim.82), calls=%async_computation.2 | async-start | bytes 589824 | tf_op jit(solution)/shard_map/all_to_all | solution.py:27
  63.7 1.1 reshape_reshape.6
  65.7 0.9 copy.160
  66.7 3.8 %all-to-all-done.2 = bf16[8,2,128,72]{2,3,1,0:T(8,128)(2,1)} async-done(((bf16[8,2,128,72]{2,3,1,0:T(8,128)(2,1)}), bf16[8,2,128,72]{2,3,1,0:T(8,128)(2,1)}, u32[]{:S(2)}, u32[]{:S(2)}) %all-to-all-start.2) | async-done | bytes 294944 | tf_op jit(solution)/shard_map/all_to_all | solution.py:27
  70.5 1.0 copy.125
  71.5 0.9 copy.127
  72.4 26.7 %all-gather.2.cloned.1.call-done = bf16[512,4096]{1,0:T(8,128)(2,1)} async-done(((bf16[8,4096]{1,0:T(8,128)(2,1)}), bf16[512,4096]{1,0:T(8,128)(2,1)}) %all-gather.2.cloned.1.call-update) | async-done | bytes 4194320 | tf_op jit(solution)/shard_map/all_gather | solution.py:11
  99.2 4.8 %fusion.55 = (bf16[512,2048]{1,0:T(8,128)(2,1)}, bf16[512,2048]{1,0:T(8,128)(2,1)}) fusion(bf16[512,4096]{1,0:T(8,128)(2,1)} %all-gather.2.cloned.1.call-done), kind=kLoop, calls=%fused_computation.79 | loop fusion | bytes 8388608 | tf_op jit(solution)/shard_map/slice | solution.py:13
  104.0 2.9 %copy.116 = bf16[512,2048]{0,1:T(8,128)(2,1)S(1)} copy(bf16[512,2048]{1,0:T(8,128)(2,1)} %get-tuple-element.22) | data formatting | bytes 4194304 | tf_op jit(solution)/shard_map/slice | solution.py:13
  106.8 2.4 %copy.117 = bf16[512,16,128]{2,0,1:T(8,128)(2,1)} copy(bf16[512,16,128]{0,2,1:T(8,128)(2,1)S(1)} %bitcast.123) | data formatting | bytes 4194304 | tf_op jit(solution)/shard_map/reshape | solution.py:13
  109.3 2.9 %copy.119 = bf16[512,2048]{0,1:T(8,128)(2,1)S(1)} copy(bf16[512,2048]{1,0:T(8,128)(2,1)} %get-tuple-element.23) | data formatting | bytes 4194304 | tf_op jit(solution)/shard_map/slice | solution.py:13
  112.1 1.7 fusion.66
  114.2 1.9 pad_maximum_fusion
  116.1 5.2 %fusion.56 = (f32[2,64,16]{2,1,0:T(8,128)S(1)}, f32[2,64,16,192]{3,2,1,0:T(8,128)}) fusion(pred[2,64,192]{2,1,0:T(8,128)(4,1)S(1)} %pad_add_fusion, bf16[2,64,16,576]{3,1,0,2:T(8,128)(2,1)} %pad_maximum_fusion, bf16[2,64,576]{2,1,0:T(8,128)(2,1)S(1)} %bitcast.134, bf16[2,128,576]{2,1,0:T(8,128)(2,1)} %copy.127), kind=kOutput, calls=%fused_computation.80 | convolution fusion | flops 455442624 | bytes 4407296 | tf_op jit(solution)/shard_map/vmap()/sub | solution.py:61
  121.3 2.0 fusion.54
  123.3 0.7 convolution_convert_fusion.1
  124.0 0.9 copy-done.1
  126.3 0.7 fusion.22
  127.0 1.3 fusion.13
  128.6 11.3 %multiply_convert_fusion.1 = bf16[2,64,16,192]{3,2,1,0:T(8,128)(2,1)S(1)} fusion(f32[2,64,16,192]{3,2,1,0:T(8,128)S(1)} %fusion.13, f32[2,64,16,192]{3,2,1,0:T(8,128)S(1)} %copy-done.4, f32[2,64,16]{2,1,0:T(8,128)S(1)} %get-tuple-element.24), kind=kOutput, calls=%fused_computation.18 | output fusion | flops 2754751 | bytes 3940352 | tf_op jit(solution)/shard_map/vmap()/sub | solution.py:73
  139.9 0.9 fusion.28
  140.8 1.0 convolution_convert_fusion
  141.8 1.8 slice.48
  145.3 0.9 copy.191
  146.4 0.8 copy.143
  147.2 9.1 %all-to-all-start.4 = ((bf16[8,2,128,72]{2,3,1,0:T(8,128)(2,1)}), bf16[8,2,128,72]{2,3,1,0:T(8,128)(2,1)S(1)}, u32[]{:S(2)}, u32[]{:S(2)}) async-start(bf16[8,2,128,72]{2,3,1,0:T(8,128)(2,1)} %copy.143), calls=%async_computation.4 | async-start | bytes 589824 | tf_op jit(solution)/shard_map/all_to_all | solution.py:41
  156.6 0.8 copy.140
  157.4 2.8 %copy.133 = bf16[2,64,16,512]{3,1,0,2:T(8,128)(2,1)S(1)} copy(bf16[2,64,16,512]{3,2,1,0:T(8,128)(2,1)} %slice.48) | data formatting | bytes 4194304 | tf_op jit(solution)/shard_map/vmap()/slice | solution.py:76
  161.4 1.6 all-to-all-done.4
  163.1 0.7 copy.145
  163.8 8.0 %all-to-all-start.5 = ((bf16[1,2,128,72]{3,1,0,2:T(2,128)(2,1)}), bf16[1,2,128,72]{3,1,0,2:T(2,128)(2,1)S(1)}, u32[]{:S(2)}, u32[]{:S(2)}) async-start(bf16[1,2,128,72]{3,1,0,2:T(2,128)(2,1)} %copy.145), calls=%async_computation.5 | async-start | bytes 131072 | tf_op jit(solution)/shard_map/all_to_all | solution.py:151
  172.7 2.0 convert_element_type.102
  174.7 8.3 %all-to-all-done.5 = bf16[1,2,128,72]{3,1,0,2:T(2,128)(2,1)S(1)} async-done(((bf16[1,2,128,72]{3,1,0,2:T(2,128)(2,1)}), bf16[1,2,128,72]{3,1,0,2:T(2,128)(2,1)S(1)}, u32[]{:S(2)}, u32[]{:S(2)}) %all-to-all-start.5) | async-done | bytes 36896 | tf_op jit(solution)/shard_map/all_to_all | solution.py:151
  183.0 5.8 %all-to-all-start.3 = ((bf16[8,128,72]{1,2,0:T(8,128)(2,1)}), bf16[8,128,72]{1,2,0:T(8,128)(2,1)S(1)}, u32[]{:S(2)}, u32[]{:S(2)}) async-start(bf16[8,128,72]{1,2,0:T(8,128)(2,1)} %copy.140), calls=%async_computation.3 | async-start | bytes 294912 | tf_op jit(solution)/shard_map/all_to_all | solution.py:41
  189.9 4.3 %all-to-all-done.3 = bf16[8,128,72]{1,2,0:T(8,128)(2,1)S(1)} async-done(((bf16[8,128,72]{1,2,0:T(8,128)(2,1)}), bf16[8,128,72]{1,2,0:T(8,128)(2,1)S(1)}, u32[]{:S(2)}, u32[]{:S(2)}) %all-to-all-start.3) | async-done | bytes 147488 | tf_op jit(solution)/shard_map/all_to_all | solution.py:41
  194.2 4.6 %all-to-all-start.6 = ((bf16[64,2,72]{2,1,0:T(2,128)(2,1)}), bf16[64,2,72]{2,1,0:T(2,128)(2,1)S(1)}, u32[]{:S(2)}, u32[]{:S(2)}) async-start(bf16[64,2,72]{2,1,0:T(2,128)(2,1)} %copy.149), calls=%async_computation.6 | async-start | bytes 65536 | tf_op jit(solution)/shard_map/all_to_all | solution.py:160
  199.5 10.1 %all-to-all-done.6 = bf16[64,2,72]{2,1,0:T(2,128)(2,1)S(1)} async-done(((bf16[64,2,72]{2,1,0:T(2,128)(2,1)}), bf16[64,2,72]{2,1,0:T(2,128)(2,1)S(1)}, u32[]{:S(2)}, u32[]{:S(2)}) %all-to-all-start.6) | async-done | bytes 18464 | tf_op jit(solution)/shard_map/all_to_all | solution.py:160
  (79 shorter events, 11.1 us)
Async XLA Ops:
  7.2 1.6 copy-start
  7.2 56.5 %copy-start.7 = (bf16[128,3072]{1,0:T(8,128)(2,1)S(1)}, bf16[128,3072]{1,0:T(8,128)(2,1)}, u32[]{:S(2)}) copy-start(bf16[128,3072]{1,0:T(8,128)(2,1)} %param.10) | copy-start | bytes 2359300
  7.2 92.0 %all-gather.2.cloned.1.call-start = ((), (), s32[]{:S(2)}) async-start(), calls=%async_computation.7 | async-start | bytes 4259840 | tf_op jit(solution)/shard_map/all_gather | solution.py:11
  9.5 28.3 %all-to-all-start = ((bf16[1,128,72]{2,0,1:T(2,128)(2,1)}), bf16[1,128,72]{2,0,1:T(2,128)(2,1)S(1)}, u32[]{:S(2)}, u32[]{:S(2)}) async-start(bf16[1,128,72]{2,0,1:T(2,128)(2,1)} %copy.159), calls=%async_computation | async-start | bytes 131072 | tf_op jit(solution)/shard_map/all_to_all | solution.py:122
  39.4 15.9 %all-to-all-start.1 = ((bf16[64,2,2,72]{3,2,1,0:T(2,128)(2,1)}), bf16[64,2,2,72]{3,2,1,0:T(2,128)(2,1)S(1)}, u32[]{:S(2)}, u32[]{:S(2)}) async-start(bf16[64,2,2,72]{3,2,1,0:T(2,128)(2,1)} %broadcast_select_fusion), calls=%async_computation.1 | async-start | bytes 131072 | tf_op jit(solution)/shard_map/all_to_all | solution.py:125
  56.1 14.4 %all-to-all-start.2 = ((bf16[8,2,128,72]{2,3,1,0:T(8,128)(2,1)}), bf16[8,2,128,72]{2,3,1,0:T(8,128)(2,1)}, u32[]{:S(2)}, u32[]{:S(2)}) async-start(bf16[8,2,128,72]{2,3,1,0:T(8,128)(2,1)} %broadcast_in_dim.82), calls=%async_computation.2 | async-start | bytes 589824 | tf_op jit(solution)/shard_map/all_to_all | solution.py:27
  63.6 1.4 copy-start.10
  63.6 1.5 copy-start.9
  63.7 1.6 copy-start.8
  121.3 2.0 copy-start.5
  123.3 1.6 copy-start.1
  127.0 1.6 copy-start.4
  128.6 11.3 %copy-start.3 = (bf16[2,64,16,576]{3,1,0,2:T(8,128)(2,1)S(1)}, bf16[2,64,16,576]{3,1,0,2:T(8,128)(2,1)}, u32[]{:S(2)}) copy-start(bf16[2,64,16,576]{3,1,0,2:T(8,128)(2,1)} %pad_maximum_fusion) | copy-start | bytes 7077892
  140.8 1.0 copy-start.6
  141.8 2.2 copy-start.2
  144.7 1.5 slice-start.2
  144.9 11.4 %slice-start.1 = ((bf16[2,192,576]{2,1,0:T(8,128)(2,1)}), bf16[2,64,576]{2,1,0:T(8,128)(2,1)S(1)}, s32[]{:S(2)}) async-start(bf16[2,192,576]{2,1,0:T(8,128)(2,1)} %copy-done.6), calls=%async_computation.9 | async-start | bytes 327680 | tf_op jit(solution)/shard_map/slice | solution.py:145
  147.2 15.9 %all-to-all-start.4 = ((bf16[8,2,128,72]{2,3,1,0:T(8,128)(2,1)}), bf16[8,2,128,72]{2,3,1,0:T(8,128)(2,1)S(1)}, u32[]{:S(2)}, u32[]{:S(2)}) async-start(bf16[8,2,128,72]{2,3,1,0:T(8,128)(2,1)} %copy.143), calls=%async_computation.4 | async-start | bytes 589824 | tf_op jit(solution)/shard_map/all_to_all | solution.py:41
  160.1 1.0 slice-start
  163.8 19.2 %all-to-all-start.5 = ((bf16[1,2,128,72]{3,1,0,2:T(2,128)(2,1)}), bf16[1,2,128,72]{3,1,0,2:T(2,128)(2,1)S(1)}, u32[]{:S(2)}, u32[]{:S(2)}) async-start(bf16[1,2,128,72]{3,1,0,2:T(2,128)(2,1)} %copy.145), calls=%async_computation.5 | async-start | bytes 131072 | tf_op jit(solution)/shard_map/all_to_all | solution.py:151
  183.0 11.2 %all-to-all-start.3 = ((bf16[8,128,72]{1,2,0:T(8,128)(2,1)}), bf16[8,128,72]{1,2,0:T(8,128)(2,1)S(1)}, u32[]{:S(2)}, u32[]{:S(2)}) async-start(bf16[8,128,72]{1,2,0:T(8,128)(2,1)} %copy.140), calls=%async_computation.3 | async-start | bytes 294912 | tf_op jit(solution)/shard_map/all_to_all | solution.py:41
  194.2 15.4 %all-to-all-start.6 = ((bf16[64,2,72]{2,1,0:T(2,128)(2,1)}), bf16[64,2,72]{2,1,0:T(2,128)(2,1)S(1)}, u32[]{:S(2)}, u32[]{:S(2)}) async-start(bf16[64,2,72]{2,1,0:T(2,128)(2,1)} %copy.149), calls=%async_computation.6 | async-start | bytes 65536 | tf_op jit(solution)/shard_map/all_to_all | solution.py:160
Sparse Core Ops, SparseCore 0:
  11.0 88.1 all-gather.1
where the time goes:
time: 218 us; the launch traced here: 217 us
  waiting for transfers between devices  74.4 us (34%)
  starting transfers between devices  56.8 us (26%)
  local copies, waits for them, and re-layouts  36.1 us (17%)
  other arithmetic  21.5 us (10%)
  between operations  14.5 us (7%)
  matrix products  13.8 us (6%)
    all_gather x1, waiting for transfers between devices, turned_gather(): out, at, done = (lax.all_gather(both, axis, axis=0, tiled=True), 0, [])  26.7 us
    all_to_all x1, starting transfers between devices, body(): lax.all_to_all(latent_share, 'resp', split_axis=1, concat_axis=0, tiled=T...  17.1 us
    all_to_all x2, starting transfers between devices, sent_and_summed(): tiles = lax.all_to_all(split_up(array, dim, length), axis, 0, 0, tiled=True)  14.9 us
    sub x1, other arithmetic, attend(): grad_weights - inner  11.3 us
    all_to_all x1, waiting for transfers between devices, body(): lax.all_to_all(outgoing, 'resp', split_axis=0, concat_axis=2, tiled=True)[0]  11.2 us
    slice x3, local copies, waits for them, and re-layouts, turned_gather(): piece = out[:, at:at + t[0].size].reshape(-1, *t.shape[1:])  10.5 us
    all_to_all x1, waiting for transfers between devices, body(): lax.all_to_all(summed.astype(jnp.bfloat16), 'resp', split_axis=0, concat_...  10.1 us
    all_to_all x1, waiting for transfers between devices, body(): lax.all_to_all(latent_share, 'resp', split_axis=1, concat_axis=0, tiled=T...  8.36 us
  transfers between devices with their start and end apart: 8, of which 8 were waited for; matrix products, arithmetic and copies ran while one was open for 9% of the time, Pallas kernels for 0%

commit v1 on v0

--- a/solution.py
+++ b/solution.py
@@ -8,7 +8,13 @@
 def turned_gather(arrays, axis, dims):
     turned = [jnp.moveaxis(a, dim, 0) for a, dim in zip(arrays, dims)]
     both = jnp.concatenate([t.reshape(len(t), -1) for t in turned], axis=1)
-    out, at, done = (lax.all_gather(both, axis, axis=0, tiled=True), 0, [])
+    out, at, done = (
+        jnp.concatenate(
+            lax.all_to_all(jnp.stack([both] * lax.axis_size(axis)), axis, 0, 0), axis=0
+        ),
+        0,
+        [],
+    )
     for t, dim in zip(turned, dims):
         piece = out[:, at : at + t[0].size].reshape(-1, *t.shape[1:])
         done.append(jnp.moveaxis(piece, 0, dim))

time: 218 us -> 306 us (1.40)
  waiting for transfers between devices: 74.4 us -> 147 us
  blocking collectives: 0 us -> 14.9 us
  starting transfers between devices: 56.8 us -> 70.6 us
  between operations: 14.5 us -> 1.15 us
    all_to_all x1, waiting for transfers between devices: 11.2 us -> 107 us  [turned_gather(): lax.all_to_all(jnp.stack([both] * lax.axis_size(axis)), axis, 0, 0)]
    all_gather x1 -> x0, waiting for transfers between devices: 26.7 us -> none  [turned_gather(): out, at, done = (lax.all_gather(both, axis, axis=0, tiled=True), 0, [])]
    all_to_all x0 -> x1, blocking collectives: none -> 14.9 us  [body(): lax.all_to_all(outgoing, 'resp', split_axis=0, concat_axis=2, tiled=True)[0]]
    all_to_all x1, starting transfers between devices: 8.03 us -> 22.2 us  [body(): lax.all_to_all(grad_prompt_rows[None].astype(jnp.bfloat16), 'resp', split...]
    unnamed x30 -> x40, local copies, waits for them, and re-layouts: 5.29 us -> 6.2 us
  transfers between devices with their start and end apart: 8 -> 7, of which waited for: 8 -> 7; matrix products, arithmetic and copies ran while one was open for 9% -> 5% of each run, Pallas kernels for 0% -> 0%
where the time goes in v1:
time: 306 us; the launch traced here: 305 us
  waiting for transfers between devices  147 us (48%)
  starting transfers between devices  70.6 us (23%)
  local copies, waits for them, and re-layouts  38.5 us (13%)
  other arithmetic  19.4 us (6%)
  blocking collectives  14.9 us (5%)
  matrix products  13.8 us (5%)
    all_to_all x1, waiting for transfers between devices, turned_gather(): lax.all_to_all(jnp.stack([both] * lax.axis_size(axis)), axis, 0, 0)  107 us
    all_to_all x1, starting transfers between devices, body(): lax.all_to_all(grad_prompt_rows[None].astype(jnp.bfloat16), 'resp', split...  22.2 us
    all_to_all x1, starting transfers between devices, body(): lax.all_to_all(latent_share, 'resp', split_axis=1, concat_axis=0, tiled=T...  17.1 us
    all_to_all x1, blocking collectives, body(): lax.all_to_all(outgoing, 'resp', split_axis=0, concat_axis=2, tiled=True)[0]  14.9 us
    all_to_all x2, starting transfers between devices, sent_and_summed(): tiles = lax.all_to_all(split_up(array, dim, length), axis, 0, 0, tiled=True)  13.2 us
    sub x1, other arithmetic, attend(): grad_weights - inner  11.3 us
    slice x3, local copies, waits for them, and re-layouts, turned_gather(): piece = out[:, at:at + t[0].size].reshape(-1, *t.shape[1:])  10.5 us
    all_to_all x1, waiting for transfers between devices, body(): lax.all_to_all(summed.astype(jnp.bfloat16), 'resp', split_axis=0, concat_...  10.1 us
  transfers between devices with their start and end apart: 7, of which 7 were waited for; matrix products, arithmetic and copies ran while one was open for 5% of the time, Pallas kernels for 0%

profile of v1, /device:TPU:1, one launch (start us, length us, event | category | flops | bytes accessed | tf_op | source)
XLA Modules:
  0.0 305.2 jit_solution(1976460120917905606)
XLA Ops:
  0.7 0.9 copy-done
  1.6 0.8 copy.159
  2.3 17.1 %all-to-all-start.1 = ((bf16[1,128,72]{2,0,1:T(2,128)(2,1)}), bf16[1,128,72]{2,0,1:T(2,128)(2,1)S(1)}, u32[]{:S(2)}, u32[]{:S(2)}) async-start(bf16[1,128,72]{2,0,1:T(2,128)(2,1)} %copy.159), calls=%async_computation.1 | async-start | bytes 131072 | tf_op jit(solution)/shard_map/all_to_all | solution.py:128
  19.4 0.7 copy.118
  21.1 0.8 select_reduce_fusion.1
  22.1 8.5 %all-to-all-done.1 = bf16[1,128,72]{2,0,1:T(2,128)(2,1)S(1)} async-done(((bf16[1,128,72]{2,0,1:T(2,128)(2,1)}), bf16[1,128,72]{2,0,1:T(2,128)(2,1)S(1)}, u32[]{:S(2)}, u32[]{:S(2)}) %all-to-all-start.1) | async-done | bytes 18464 | tf_op jit(solution)/shard_map/all_to_all | solution.py:128
  30.6 0.7 gather_fusion
  31.5 14.9 %all_to_all.71 = bf16[64,2,2,72]{3,2,1,0:T(2,128)(2,1)S(1)} all-to-all(bf16[64,2,2,72]{3,2,1,0:T(2,128)(2,1)S(1)} %broadcast_select_fusion), channel_id=1, replica_groups=mesh['resp'=64,'head'=8] {'resp'}, dimensions={0} | all-to-all | bytes 73728 | tf_op jit(solution)/shard_map/all_to_all | solution.py:131
  46.6 0.8 broadcast_in_dim.82
  47.3 7.6 %all-to-all-start.3 = ((bf16[8,2,128,72]{2,3,1,0:T(8,128)(2,1)}), bf16[8,2,128,72]{2,3,1,0:T(8,128)(2,1)S(1)}, u32[]{:S(2)}, u32[]{:S(2)}) async-start(bf16[8,2,128,72]{2,3,1,0:T(8,128)(2,1)} %broadcast_in_dim.82), calls=%async_computation.3 | async-start | bytes 589824 | tf_op jit(solution)/shard_map/all_to_all | solution.py:33
  54.9 6.8 %all-to-all-done.3 = bf16[8,2,128,72]{2,3,1,0:T(8,128)(2,1)S(1)} async-done(((bf16[8,2,128,72]{2,3,1,0:T(8,128)(2,1)}), bf16[8,2,128,72]{2,3,1,0:T(8,128)(2,1)S(1)}, u32[]{:S(2)}, u32[]{:S(2)}) %all-to-all-start.3) | async-done | bytes 294944 | tf_op jit(solution)/shard_map/all_to_all | solution.py:33
  61.7 2.5 stack.2
  64.2 6.0 %all-to-all-start = ((bf16[64,8,4096]{2,1,0:T(8,128)(2,1)}), bf16[64,8,4096]{2,1,0:T(8,128)(2,1)}, u32[]{:S(2)}, u32[]{:S(2)}) async-start(bf16[64,8,4096]{2,1,0:T(8,128)(2,1)} %stack.2), calls=%async_computation | async-start | bytes 8388608 | tf_op jit(solution)/shard_map/all_to_all | solution.py:13
  70.2 1.1 reshape_reshape.6
  72.3 0.9 copy.160
  73.5 0.9 copy.127
  74.4 107.3 %all-to-all-done = bf16[64,8,4096]{2,1,0:T(8,128)(2,1)} async-done(((bf16[64,8,4096]{2,1,0:T(8,128)(2,1)}), bf16[64,8,4096]{2,1,0:T(8,128)(2,1)}, u32[]{:S(2)}, u32[]{:S(2)}) %all-to-all-start) | async-done | bytes 4194336 | tf_op jit(solution)/shard_map/all_to_all | solution.py:13
  181.6 4.8 %fusion.55 = (bf16[512,2048]{1,0:T(8,128)(2,1)}, bf16[512,2048]{1,0:T(8,128)(2,1)}) fusion(bf16[512,4096]{1,0:T(8,128)(2,1)} %bitcast.4), kind=kLoop, calls=%fused_computation.79 | loop fusion | bytes 8388608 | tf_op jit(solution)/shard_map/slice | solution.py:19
  186.4 2.9 copy.116
  189.3 2.4 copy.117
  191.7 2.9 copy.119
  194.6 1.7 fusion.66
  196.7 1.9 pad_maximum_fusion
  198.6 5.2 %fusion.56 = (f32[2,64,16]{2,1,0:T(8,128)S(1)}, f32[2,64,16,192]{3,2,1,0:T(8,128)}) fusion(pred[2,64,192]{2,1,0:T(8,128)(4,1)S(1)} %pad_add_fusion, bf16[2,64,16,576]{3,1,0,2:T(8,128)(2,1)} %pad_maximum_fusion, bf16[2,64,576]{2,1,0:T(8,128)(2,1)S(1)} %bitcast.135, bf16[2,128,576]{2,1,0:T(8,128)(2,1)} %copy.127), kind=kOutput, calls=%fused_computation.80 | convolution fusion | flops 455442624 | bytes 4407296 | tf_op jit(solution)/shard_map/vmap()/sub | solution.py:67
  203.8 2.0 fusion.54
  205.8 0.7 convolution_convert_fusion.1
  206.5 0.9 copy-done.2
  207.4 0.7 fusion.7
  208.8 0.7 fusion.22
  209.5 1.3 fusion.13
  211.1 11.3 %multiply_convert_fusion.1 = bf16[2,64,16,192]{3,2,1,0:T(8,128)(2,1)S(1)} fusion(f32[2,64,16,192]{3,2,1,0:T(8,128)S(1)} %fusion.13, f32[2,64,16,192]{3,2,1,0:T(8,128)S(1)} %copy-done.5, f32[2,64,16]{2,1,0:T(8,128)S(1)} %get-tuple-element.24), kind=kOutput, calls=%fused_computation.18 | output fusion | flops 2754751 | bytes 3940352 | tf_op jit(solution)/shard_map/vmap()/sub | solution.py:79
  222.3 0.9 fusion.28
  223.3 1.0 convolution_convert_fusion
  224.3 1.8 slice.48
  227.7 0.9 copy.191
  228.9 0.8 copy.143
  229.6 7.4 %all-to-all-start.5 = ((bf16[8,2,128,72]{2,3,1,0:T(8,128)(2,1)}), bf16[8,2,128,72]{2,3,1,0:T(8,128)(2,1)S(1)}, u32[]{:S(2)}, u32[]{:S(2)}) async-start(bf16[8,2,128,72]{2,3,1,0:T(8,128)(2,1)} %copy.143), calls=%async_computation.5 | async-start | bytes 589824 | tf_op jit(solution)/shard_map/all_to_all | solution.py:47
  237.3 0.9 copy.140
  238.2 2.8 copy.133
  242.2 1.6 all-to-all-done.5
  243.9 0.7 copy.145
  244.6 22.2 %all-to-all-start.6 = ((bf16[1,2,128,72]{3,1,0,2:T(2,128)(2,1)}), bf16[1,2,128,72]{3,1,0,2:T(2,128)(2,1)S(1)}, u32[]{:S(2)}, u32[]{:S(2)}) async-start(bf16[1,2,128,72]{3,1,0,2:T(2,128)(2,1)} %copy.145), calls=%async_computation.6 | async-start | bytes 131072 | tf_op jit(solution)/shard_map/all_to_all | solution.py:157
  267.7 2.0 convert_element_type.102
  269.7 8.2 %all-to-all-done.6 = bf16[1,2,128,72]{3,1,0,2:T(2,128)(2,1)S(1)} async-done(((bf16[1,2,128,72]{3,1,0,2:T(2,128)(2,1)}), bf16[1,2,128,72]{3,1,0,2:T(2,128)(2,1)S(1)}, u32[]{:S(2)}, u32[]{:S(2)}) %all-to-all-start.6) | async-done | bytes 36896 | tf_op jit(solution)/shard_map/all_to_all | solution.py:157
  277.9 5.8 %all-to-all-start.4 = ((bf16[8,128,72]{1,2,0:T(8,128)(2,1)}), bf16[8,128,72]{1,2,0:T(8,128)(2,1)S(1)}, u32[]{:S(2)}, u32[]{:S(2)}) async-start(bf16[8,128,72]{1,2,0:T(8,128)(2,1)} %copy.140), calls=%async_computation.4 | async-start | bytes 294912 | tf_op jit(solution)/shard_map/all_to_all | solution.py:47
  284.8 4.3 %all-to-all-done.4 = bf16[8,128,72]{1,2,0:T(8,128)(2,1)S(1)} async-done(((bf16[8,128,72]{1,2,0:T(8,128)(2,1)}), bf16[8,128,72]{1,2,0:T(8,128)(2,1)S(1)}, u32[]{:S(2)}, u32[]{:S(2)}) %all-to-all-start.4) | async-done | bytes 147488 | tf_op jit(solution)/shard_map/all_to_all | solution.py:47
  289.1 4.6 %all-to-all-start.7 = ((bf16[64,2,72]{2,1,0:T(2,128)(2,1)}), bf16[64,2,72]{2,1,0:T(2,128)(2,1)S(1)}, u32[]{:S(2)}, u32[]{:S(2)}) async-start(bf16[64,2,72]{2,1,0:T(2,128)(2,1)} %copy.149), calls=%async_computation.7 | async-start | bytes 65536 | tf_op jit(solution)/shard_map/all_to_all | solution.py:166
  294.4 10.1 %all-to-all-done.7 = bf16[64,2,72]{2,1,0:T(2,128)(2,1)S(1)} async-done(((bf16[64,2,72]{2,1,0:T(2,128)(2,1)}), bf16[64,2,72]{2,1,0:T(2,128)(2,1)S(1)}, u32[]{:S(2)}, u32[]{:S(2)}) %all-to-all-start.7) | async-done | bytes 18464 | tf_op jit(solution)/shard_map/all_to_all | solution.py:166
  (88 shorter events, 10.6 us)
Async XLA Ops:
  0.6 0.9 copy-start
  0.6 54.3 %copy-start.13 = (bf16[16,8,128]{2,1,0:T(8,128)(2,1)S(1)}, bf16[16,8,128]{2,1,0:T(8,128)(2,1)}, u32[]{:S(2)}) copy-start(bf16[16,8,128]{2,1,0:T(8,128)(2,1)} %param.14) | copy-start | bytes 98308
  0.7 54.2 %copy-start.14 = (bf16[16,128,8]{1,2,0:T(8,128)(2,1)S(1)}, bf16[16,128,8]{1,2,0:T(8,128)(2,1)}, u32[]{:S(2)}) copy-start(bf16[16,128,8]{1,2,0:T(8,128)(2,1)} %param.13) | copy-start | bytes 98308
  2.3 28.3 %all-to-all-start.1 = ((bf16[1,128,72]{2,0,1:T(2,128)(2,1)}), bf16[1,128,72]{2,0,1:T(2,128)(2,1)S(1)}, u32[]{:S(2)}, u32[]{:S(2)}) async-start(bf16[1,128,72]{2,0,1:T(2,128)(2,1)} %copy.159), calls=%async_computation.1 | async-start | bytes 131072 | tf_op jit(solution)/shard_map/all_to_all | solution.py:128
  47.3 14.3 %all-to-all-start.3 = ((bf16[8,2,128,72]{2,3,1,0:T(8,128)(2,1)}), bf16[8,2,128,72]{2,3,1,0:T(8,128)(2,1)S(1)}, u32[]{:S(2)}, u32[]{:S(2)}) async-start(bf16[8,2,128,72]{2,3,1,0:T(8,128)(2,1)} %broadcast_in_dim.82), calls=%async_computation.3 | async-start | bytes 589824 | tf_op jit(solution)/shard_map/all_to_all | solution.py:33
  61.7 2.5 copy-start.8
  64.2 6.0 %copy-start.10 = (bf16[128,3072]{1,0:T(8,128)(2,1)S(1)}, bf16[128,3072]{1,0:T(8,128)(2,1)}, u32[]{:S(2)}) copy-start(bf16[128,3072]{1,0:T(8,128)(2,1)} %param.10) | copy-start | bytes 2359300
  64.2 117.5 %all-to-all-start = ((bf16[64,8,4096]{2,1,0:T(8,128)(2,1)}), bf16[64,8,4096]{2,1,0:T(8,128)(2,1)}, u32[]{:S(2)}, u32[]{:S(2)}) async-start(bf16[64,8,4096]{2,1,0:T(8,128)(2,1)} %stack.2), calls=%async_computation | async-start | bytes 8388608 | tf_op jit(solution)/shard_map/all_to_all | solution.py:13
  70.2 1.4 copy-start.15
  70.2 1.5 copy-start.12
  70.2 1.7 copy-start.11
  71.9 1.6 copy-start.9
  203.8 2.0 copy-start.6
  205.8 1.6 copy-start.2
  209.5 1.6 copy-start.5
  211.1 11.3 %copy-start.4 = (bf16[2,64,16,576]{3,1,0,2:T(8,128)(2,1)S(1)}, bf16[2,64,16,576]{3,1,0,2:T(8,128)(2,1)}, u32[]{:S(2)}) copy-start(bf16[2,64,16,576]{3,1,0,2:T(8,128)(2,1)} %pad_maximum_fusion) | copy-start | bytes 7077892
  223.3 1.0 copy-start.7
  224.3 2.2 copy-start.3
  227.2 1.5 slice-start.2
  227.4 9.7 %slice-start.1 = ((bf16[2,192,576]{2,1,0:T(8,128)(2,1)}), bf16[2,64,576]{2,1,0:T(8,128)(2,1)S(1)}, s32[]{:S(2)}) async-start(bf16[2,192,576]{2,1,0:T(8,128)(2,1)} %copy-done.7), calls=%async_computation.9 | async-start | bytes 327680 | tf_op jit(solution)/shard_map/slice | solution.py:151
  229.6 14.2 %all-to-all-start.5 = ((bf16[8,2,128,72]{2,3,1,0:T(8,128)(2,1)}), bf16[8,2,128,72]{2,3,1,0:T(8,128)(2,1)S(1)}, u32[]{:S(2)}, u32[]{:S(2)}) async-start(bf16[8,2,128,72]{2,3,1,0:T(8,128)(2,1)} %copy.143), calls=%async_computation.5 | async-start | bytes 589824 | tf_op jit(solution)/shard_map/all_to_all | solution.py:47
  240.9 1.0 slice-start
  244.6 33.3 %all-to-all-start.6 = ((bf16[1,2,128,72]{3,1,0,2:T(2,128)(2,1)}), bf16[1,2,128,72]{3,1,0,2:T(2,128)(2,1)S(1)}, u32[]{:S(2)}, u32[]{:S(2)}) async-start(bf16[1,2,128,72]{3,1,0,2:T(2,128)(2,1)} %copy.145), calls=%async_computation.6 | async-start | bytes 131072 | tf_op jit(solution)/shard_map/all_to_all | solution.py:157
  267.1 38.2 %copy-start.1 = (bf16[1,128,576]{1,2,0:T(8,128)(2,1)S(1)}, bf16[1,128,576]{1,2,0:T(8,128)(2,1)}, u32[]{:S(2)}) copy-start(bf16[1,128,576]{1,2,0:T(8,128)(2,1)} %param.12) | copy-start | bytes 442372
  277.9 11.2 %all-to-all-start.4 = ((bf16[8,128,72]{1,2,0:T(8,128)(2,1)}), bf16[8,128,72]{1,2,0:T(8,128)(2,1)S(1)}, u32[]{:S(2)}, u32[]{:S(2)}) async-start(bf16[8,128,72]{1,2,0:T(8,128)(2,1)} %copy.140), calls=%async_computation.4 | async-start | bytes 294912 | tf_op jit(solution)/shard_map/all_to_all | solution.py:47
  289.1 15.4 %all-to-all-start.7 = ((bf16[64,2,72]{2,1,0:T(2,128)(2,1)}), bf16[64,2,72]{2,1,0:T(2,128)(2,1)S(1)}, u32[]{:S(2)}, u32[]{:S(2)}) async-start(bf16[64,2,72]{2,1,0:T(2,128)(2,1)} %copy.149), calls=%async_computation.7 | async-start | bytes 65536 | tf_op jit(solution)/shard_map/all_to_all | solution.py:166
